TPU v7x, 32 devices: a whole 2x2x4 slice. The times are simulated.
32 devices in a mesh: row: 8 (over z, y), col: 4 (over x, core).
Axes of the slice: x: 2, y: 2, z: 4, core: 2. Of those that a mesh axis runs over, the one named last changes fastest.
Arguments:
- params: float32 [4, 4096, 10240], P(None, ('row', 'col'))
- grads: bfloat16 [4, 4096, 10240], P(None, ('row', 'col')), may hold values from -6 to 6
- row_state_old: float32 [4, 4096], P(None, ('row', 'col')), may hold values from 0.05 to 0.5
- col_state_old: float32 [4, 10240], P(None, ('row', 'col')), may hold values from 0.05 to 0.5
- old_map: int32 [4, 32], replicated, may hold values from 0 to 31, each once within a row
- new_map: int32 [4, 32], replicated, may hold values from 0 to 31, each once within a row
Outputs:
- new_params: float32 [4, 4096, 10240], P(None, 'row', 'col')
- step_change: float32 [4, 4096, 10240], P(None, 'row', 'col')
- row_state: float32 [4, 4096], P(None, ('row', 'col'))
- col_state: float32 [4, 10240], P(None, ('row', 'col'))
Inputs may be any that keep to these rules, and one draw needn't show every extreme that they name: Each row of old_map is a permutation of 0 to 31. Each row of new_map is a permutation of 0 to 31.
All inputs are finite; a program needn't handle non-finite values.
Results may differ from a plain program's by a relative error of at most 0.0003.
Values may be sent and summed in bfloat16 or wider, within the bound.
No kernel may reach another device: no remote copies, remote signals or barrier semaphores. Data moves between devices by JAX's collectives and lax.ppermute only.
A program may use at most 192 MiB of HBM per device.

v0:
```python
import math
import jax
import jax.numpy as jnp
from jax import lax
from jax.sharding import PartitionSpec as P

D = 4096
FF = 10240
STEP = 4
eps_square = 1e-30
clip_limit = 1.0
highest = lax.Precision.HIGHEST


def reorder(stored, order, blocks):
    matrices = stored.shape[0]
    pieces = stored.reshape(matrices, blocks, stored.shape[1] // blocks)
    onehot = (order[:, :, None] == jnp.arange(blocks, dtype=jnp.int32)[None, None, :]).astype(
        jnp.float32
    )
    return jnp.einsum("mfb,mfw->mbw", onehot, pieces, precision=highest).reshape(matrices, -1)


def select_block(whole, order, blocks, flat_index):
    matrices = whole.shape[0]
    wanted = lax.dynamic_slice_in_dim(order, flat_index, 1, 1)
    onehot = (wanted == jnp.arange(blocks, dtype=jnp.int32)[None, :]).astype(jnp.float32)
    pieces = whole.reshape(matrices, blocks, whole.shape[1] // blocks)
    return jnp.einsum("mb,mbw->mw", onehot, pieces, precision=highest)


def totals(update_part, param_part):
    param_total = lax.psum(param_part, ("row", "col"))
    update_total = lax.psum(update_part, ("row", "col"))
    return (update_total, param_total)


def apply_update(weights, gradient, row_new, col_new, row_mean, step_rate):
    variance = row_new[:, :, None] * col_new[:, None, :] / row_mean[:, None, None]
    update = gradient / jnp.sqrt(variance)
    param_part = jnp.sum(weights * weights, axis=(1, 2))
    update_part = jnp.sum(update * update, axis=(1, 2))
    update_total, param_total = totals(update_part, param_part)
    count = weights.shape[0] * D * FF
    clip_factor = jnp.maximum(1.0, jnp.sqrt(jnp.sum(update_total) / count) / clip_limit)
    param_scale = jnp.sqrt(param_total / (D * FF) + 1e-06)
    change = -(step_rate * param_scale)[:, None, None] * update / clip_factor
    return (weights + change, change)


def shards(params, grads, row_state_old, col_state_old, old_map, new_map):
    decay_rate = 1.0 - float(STEP) ** (-0.8)
    step_rate = min(0.01, 1.0 / math.sqrt(STEP))
    row_count = lax.axis_size("row")
    col_count = lax.axis_size("col")
    blocks = row_count * col_count
    flat_index = lax.axis_index(("row", "col"))
    stored_rows, stored_cols = (
        lax.all_gather(row_state_old, ("row", "col"), axis=1, tiled=True),
        lax.all_gather(col_state_old, ("row", "col"), axis=1, tiled=True),
    )
    row_old = reorder(stored_rows, old_map, blocks)
    col_old = reorder(stored_cols, old_map, blocks)
    old_mean = jnp.mean(row_old, axis=1)
    weights = lax.all_to_all(params, "col", split_axis=2, concat_axis=1, tiled=True)
    moved = lax.all_to_all(grads, "col", split_axis=2, concat_axis=1, tiled=True)
    gradient = moved.astype(jnp.float32)
    squares = gradient * gradient + eps_square
    rows_here = gradient.shape[1]
    cols_here = gradient.shape[2]
    row_total = lax.psum(jnp.sum(squares, axis=2), "col")
    col_total, grand_total = lax.psum((jnp.sum(squares, axis=1), jnp.sum(row_total, axis=1)), "row")
    row_block = lax.dynamic_slice_in_dim(row_old, lax.axis_index("row") * rows_here, rows_here, 1)
    col_block = lax.dynamic_slice_in_dim(col_old, lax.axis_index("col") * cols_here, cols_here, 1)
    row_new = decay_rate * row_block + (1.0 - decay_rate) * row_total / FF
    col_new = decay_rate * col_block + (1.0 - decay_rate) * col_total / D
    row_mean = decay_rate * old_mean + (1.0 - decay_rate) * grand_total / (D * FF)
    new_params, step_change = apply_update(weights, gradient, row_new, col_new, row_mean, step_rate)
    whole_rows = lax.all_gather(row_new, "row", axis=1, tiled=True)
    whole_cols = lax.all_gather(col_new, "col", axis=1, tiled=True)
    row_state = select_block(whole_rows, new_map, blocks, flat_index)
    col_state = select_block(whole_cols, new_map, blocks, flat_index)
    return (new_params, step_change, row_state, col_state)


def solution(mesh):
    placed = (
        P(None, ("row", "col"), None),
        P(None, ("row", "col"), None),
        P(None, ("row", "col")),
        P(None, ("row", "col")),
        P(),
        P(),
    )
    return jax.shard_map(
        shards,
        mesh=mesh,
        in_specs=placed,
        out_specs=(
            P(None, "row", "col"),
            P(None, "row", "col"),
            P(None, ("row", "col")),
            P(None, ("row", "col")),
        ),
        check_vma=False,
    )
```

profile of v0, /device:TPU:0, one launch (start us, length us, event | category | flops | bytes accessed | tf_op | source)
XLA Modules:
  0.0 772.3 jit_solution(8924082937951834836)
XLA Ops:
  0.6 0.0 copy-start
  0.6 16.7 %copy.24 = bf16[4,128,10240]{1,0,2:T(4,128)(2,1)} copy(bf16[4,128,10240]{2,1,0:T(8,128)(2,1)} %param.7) | data formatting | bytes 20971520 | tf_op args[1]
  17.4 6.0 all-to-all-start.1
  23.4 23.8 %copy.22 = f32[4,128,10240]{1,0,2:T(4,128)} copy(f32[4,128,10240]{2,1,0:T(8,128)} %param.6) | data formatting | bytes 41943040 | tf_op args[0]
  47.2 0.0 copy-start.4
  47.2 0.0 copy-start.2
  47.2 0.0 copy-start.3
  47.2 92.4 %all-to-all-done.1 = bf16[4,128,10240]{1,0,2:T(4,128)(2,1)} async-done(((bf16[4,128,10240]{1,0,2:T(4,128)(2,1)}), bf16[4,128,10240]{1,0,2:T(4,128)(2,1)}, u32[]{:S(2)}, u32[]{:S(2)}) %all-to-all-start.1) | async-done | bytes 10485792 | tf_op jit(solution)/shard_map/all_to_all | solution.py:66
  139.6 7.7 all-to-all-start
  147.3 0.0 copy-done.4
  147.3 261.9 %all_gather.12 = f32[4,4096]{1,0:T(4,128)S(1)} all-gather(f32[4,128]{1,0:T(4,128)S(1)} %copy-done.4), channel_id=1, replica_groups=mesh['row'=8,'col'=4] {'row','col'}, dimensions={1}, use_global_device_ids=true | all-gather | bytes 67584 | tf_op jit(solution)/shard_map/all_gather | solution.py:59
  409.2 0.0 copy-done.2
  409.2 0.3 fusion.18
  409.5 0.0 copy-done.3
  409.5 37.2 %all-gather = f32[32,320,4]{1,2,0:T(4,128)S(1)} all-gather(f32[1,320,4]{1,2,0:T(4,128)S(1)} %bitcast.64), channel_id=1, replica_groups=mesh['row'=8,'col'=4] {'row','col'}, dimensions={0}, use_global_device_ids=true | all-gather | bytes 168960 | tf_op jit(solution)/shard_map/all_gather | solution.py:60
  446.7 0.1 reshape.50
  446.9 0.1 reshape.42
  447.0 0.2 fusion.10
  447.2 3.2 copy.34
  450.4 0.0 copy-done
  450.4 0.2 dynamic-slice_reduce_fusion
  450.6 0.1 fusion.16
  450.7 15.4 %fusion.2 = (f32[4,2560]{0,1:T(8,128)S(1)}, f32[4,4,128]{2,0,1:T(4,128)S(1)}) fusion(bf16[4,128,4,2560]{1,0,3,2:T(4,128)(2,1)} %bitcast.7), kind=kLoop, calls=%fused_computation.8 | loop fusion | flops 26202112 | bytes 10534912 | tf_op jit(solution)/shard_map/reduce_sum | solution.py:72
  466.1 7.4 psum.36
  473.5 0.1 multiply_add_fusion.2
  473.6 73.3 %all-reduce.1 = (f32[4]{0:T(128)S(1)}, f32[4,2560]{0,1:T(8,128)S(1)}) all-reduce(f32[4]{0:T(128)S(1)} %get-tuple-element.13, f32[4,2560]{0,1:T(8,128)S(1)} %get-tuple-element.4), channel_id=1, replica_groups=mesh['row'=8,'col'=4] {'row'}, use_global_device_ids=true, to_apply=%region_8.0 | all-reduce | flops 10244 | bytes 81952 | tf_op jit(solution)/shard_map/psum | solution.py:72
  546.9 1.6 multiply_add_fusion.1
  548.5 0.4 copy.28
  548.9 32.1 %all_gather.15 = f32[4,10240]{0,1:T(8,128)} all-gather(f32[4,2560]{0,1:T(8,128)S(1)} %multiply_add_fusion.1), channel_id=1, replica_groups=mesh['row'=8,'col'=4] {'col'}, dimensions={1}, use_global_device_ids=true | all-gather | bytes 204800 | tf_op jit(solution)/shard_map/all_gather | solution.py:80
  581.0 3.6 copy.32
  584.6 0.2 fusion.13
  584.8 0.6 copy.55
  585.4 11.3 %convert_bitcast_fusion = f32[4,4,128,2560]{2,0,3,1:T(4,128)} fusion(bf16[4,128,4,2560]{1,0,3,2:T(4,128)(2,1)} %bitcast.7), kind=kLoop, calls=%fused_computation | loop fusion | flops 5242880 | bytes 31457280 | tf_op jit(solution)/shard_map/convert_element_type | solution.py:67
  596.7 23.9 %copy.25 = f32[4,4,128,2560]{3,2,1,0:T(8,128)} copy(f32[4,4,128,2560]{2,0,3,1:T(4,128)} %convert_bitcast_fusion) | data formatting | bytes 41943040 | tf_op jit(solution)/shard_map/convert_element_type | solution.py:67
  620.6 30.5 %all_gather.14 = f32[4,4096]{1,0:T(4,128)S(1)} all-gather(f32[4,512]{1,0:T(4,128)S(1)} %get-tuple-element.12), channel_id=1, replica_groups=mesh['row'=8,'col'=4] {'row'}, dimensions={1}, use_global_device_ids=true | all-gather | bytes 73728 | tf_op jit(solution)/shard_map/all_gather | solution.py:79
  651.2 0.7 fusion.4
  651.9 13.1 %multiply_reduce_fusion = f32[4]{0:T(128)S(1)} fusion(bf16[4,128,4,2560]{1,0,3,2:T(4,128)(2,1)} %bitcast.7, f32[4]{0:T(128)S(1)} %multiply_add_fusion.3, f32[4,2560]{0,1:T(8,128)S(1)} %multiply_add_fusion.1, f32[4,4,128]{2,0,1:T(4,128)S(1)} %bitcast.61), kind=kLoop, calls=%fused_computation.5 | loop fusion | flops 31457276 | bytes 10534944 | tf_op jit(solution)/shard_map/reduce_sum | solution.py:42
  665.0 0.0 all-to-all-done
  665.0 12.6 %multiply_reduce_fusion.1 = f32[4]{0:T(128)S(1)} fusion(f32[4,4,128,2560]{2,0,3,1:T(4,128)} %bitcast.1), kind=kLoop, calls=%fused_computation.7 | loop fusion | flops 10485756 | bytes 20971536 | tf_op jit(solution)/shard_map/reduce_sum | solution.py:41
  677.7 23.9 %copy.23 = f32[4,4,128,2560]{3,2,1,0:T(8,128)} copy(f32[4,4,128,2560]{2,0,3,1:T(4,128)} %bitcast.1) | data formatting | bytes 41943040 | tf_op jit(solution)/shard_map/all_to_all | solution.py:65
  701.6 39.7 %all-reduce = (f32[4]{0:T(128)S(1)}, f32[4]{0:T(128)S(1)}) all-reduce(f32[4]{0:T(128)S(1)} %multiply_reduce_fusion, f32[4]{0:T(128)S(1)} %multiply_reduce_fusion.1), channel_id=1, replica_groups=mesh['row'=8,'col'=4] {'row','col'}, use_global_device_ids=true, to_apply=%region_10.0 | all-reduce | flops 8 | bytes 64 | tf_op jit(solution)/shard_map/psum | solution.py:34
  741.3 0.6 reduce_sum.72
  742.6 0.0 copy-start.1
  742.7 29.6 %bitcast_add_fusion = (f32[4,512,2560]{2,1,0:T(8,128)}, f32[4,512,2560]{2,1,0:T(8,128)}) fusion(f32[4,4,128,2560]{3,2,1,0:T(8,128)} %copy.23, f32[]{:T(128)S(6)} %max.3, f32[4]{0:T(128)S(1)} %multiply_add_fusion.3, f32[4,2560]{1,0:T(4,128)S(1)} %copy.28, f32[4,512]{1,0:T(4,128)S(1)} %get-tuple-element.12, f32[4,4,128,2560]{3,2,1,0:T(8,128)} %copy.25, ...), kind=kLoop, calls=%fused_computation.4 | loop fusion | flops 31457280 | bytes 83935264 | tf_op jit(solution)/shard_map/add | solution.py:48
  772.3 0.0 copy-done.1
  (4 shorter events, 0.1 us)
Async XLA Ops:
  0.6 449.8 %copy-start = (s32[4,32]{1,0:T(4,128)S(1)}, s32[4,32]{1,0:T(4,128)}, u32[]{:S(2)}) copy-start(s32[4,32]{1,0:T(4,128)} %param.11) | copy-start | bytes 1540
  17.4 122.2 %all-to-all-start.1 = ((bf16[4,128,10240]{1,0,2:T(4,128)(2,1)}), bf16[4,128,10240]{1,0,2:T(4,128)(2,1)}, u32[]{:S(2)}, u32[]{:S(2)}) async-start(bf16[4,128,10240]{1,0,2:T(4,128)(2,1)} %copy.24), calls=%async_computation.1 | async-start | bytes 20971520 | tf_op jit(solution)/shard_map/all_to_all | solution.py:66
  47.2 100.2 %copy-start.4 = (f32[4,128]{1,0:T(4,128)S(1)}, f32[4,128]{1,0:T(4,128)}, u32[]{:S(2)}) copy-start(f32[4,128]{1,0:T(4,128)} %param.8) | copy-start | bytes 6148
  47.2 362.0 %copy-start.2 = (s32[4,32]{1,0:T(4,128)S(1)}, s32[4,32]{1,0:T(4,128)}, u32[]{:S(2)}) copy-start(s32[4,32]{1,0:T(4,128)} %param.10) | copy-start | bytes 1540
  47.2 362.3 %copy-start.3 = (f32[4,320]{1,0:T(4,128)S(1)}, f32[4,320]{1,0:T(4,128)}, u32[]{:S(2)}) copy-start(f32[4,320]{1,0:T(4,128)} %param.9) | copy-start | bytes 15364
  139.6 525.5 %all-to-all-start = ((f32[4,128,10240]{1,0,2:T(4,128)}), f32[4,128,10240]{1,0,2:T(4,128)}, u32[]{:S(2)}, u32[]{:S(2)}) async-start(f32[4,128,10240]{1,0,2:T(4,128)} %copy.22), calls=%async_computation | async-start | bytes 41943040 | tf_op jit(solution)/shard_map/all_to_all | solution.py:65
  742.6 29.6 %copy-start.1 = (s32[4,32]{1,0:T(4,128)S(1)}, s32[4,32]{1,0:T(4,128)}, u32[]{:S(2)}) copy-start(s32[4,32]{1,0:T(4,128)} %param.11) | copy-start | bytes 1540
where the time goes:
time: 775 us; the launch traced here: 772 us
  blocking collectives  482 us (62%)
  local copies, waits for them, and re-layouts  96.7 us (12%)
  waiting for transfers between devices  92.4 us (12%)
  other arithmetic  84.5 us (11%)
  starting transfers between devices  13.7 us (2%)
    all_gather x1, blocking collectives, shards(): lax.all_gather(row_state_old, ('row', 'col'), axis=1, tiled=True)  262 us
    all_to_all x1, waiting for transfers between devices, shards(): lax.all_to_all(grads, 'col', split_axis=2, concat_axis=1, tiled=True)  92.4 us
    psum x1, blocking collectives, shards(): lax.psum((jnp.sum(squares, axis=1), jnp.sum(row_total, axis=1)), 'row')  73.3 us
    unnamed x14, local copies, waits for them, and re-layouts  40.7 us
    psum x1, blocking collectives, totals(): update_total = lax.psum(update_part, ('row', 'col'))  39.7 us
    all_gather x1, blocking collectives, shards(): lax.all_gather(col_state_old, ('row', 'col'), axis=1, tiled=True)  37.2 us
    all_gather x1, blocking collectives, shards(): whole_cols = lax.all_gather(col_new, 'col', axis=1, tiled=True)  32.1 us
    all_gather x1, blocking collectives, shards(): whole_rows = lax.all_gather(row_new, 'row', axis=1, tiled=True)  30.5 us
  transfers between devices with their start and end apart: 2, of which 1 were waited for; matrix products, arithmetic and copies ran while one was open for 13% of the time, Pallas kernels for 0%

commit v1 on v0

--- a/solution.py
+++ b/solution.py
@@ -63,7 +63,10 @@
     col_old = reorder(stored_cols, old_map, blocks)
     old_mean = jnp.mean(row_old, axis=1)
     weights = lax.all_to_all(params, "col", split_axis=2, concat_axis=1, tiled=True)
-    moved = lax.all_to_all(grads, "col", split_axis=2, concat_axis=1, tiled=True)
+    moved = jnp.concatenate(
+        lax.all_to_all(jnp.stack(jnp.split(grads, lax.axis_size("col"), axis=2)), "col", 0, 0),
+        axis=1,
+    )
     gradient = moved.astype(jnp.float32)
     squares = gradient * gradient + eps_square
     rows_here = gradient.shape[1]

time: 775 us -> 675 us (0.87)
  blocking collectives: 482 us -> 413 us
  local copies, waits for them, and re-layouts: 96.7 us -> 70.2 us
    psum x1, blocking collectives: 73.3 us -> 33.8 us  [shards(): lax.psum((jnp.sum(squares, axis=1), jnp.sum(row_total, axis=1)), 'row')]
    all_gather x1, blocking collectives: 32.1 us -> 5.51 us  [shards(): whole_cols = lax.all_gather(col_new, 'col', axis=1, tiled=True)]
    unnamed x14 -> x13, local copies, waits for them, and re-layouts: 40.7 us -> 24 us
  transfers between devices with their start and end apart: 2 -> 2, of which waited for: 1 -> 1; matrix products, arithmetic and copies ran while one was open for 13% -> 11% of each run, Pallas kernels for 0% -> 0%
where the time goes in v1:
time: 675 us; the launch traced here: 673 us
  blocking collectives  413 us (61%)
  waiting for transfers between devices  92.4 us (14%)
  other arithmetic  80.4 us (12%)
  local copies, waits for them, and re-layouts  70.2 us (10%)
  starting transfers between devices  13.7 us (2%)
    all_gather x1, blocking collectives, shards(): lax.all_gather(row_state_old, ('row', 'col'), axis=1, tiled=True)  262 us
    all_to_all x1, waiting for transfers between devices, shards(): lax.all_to_all(jnp.stack(jnp.split(grads, lax.axis_size('col'), axis=2)),...  92.4 us
    all_gather x1, blocking collectives, shards(): lax.all_gather(col_state_old, ('row', 'col'), axis=1, tiled=True)  37.2 us
    psum x1, blocking collectives, totals(): update_total = lax.psum(update_part, ('row', 'col'))  36.8 us
    psum x1, blocking collectives, shards(): lax.psum((jnp.sum(squares, axis=1), jnp.sum(row_total, axis=1)), 'row')  33.8 us
    all_gather x1, blocking collectives, shards(): whole_rows = lax.all_gather(row_new, 'row', axis=1, tiled=True)  30.7 us
    add x1, other arithmetic, apply_update(): return (weights + change, change)  29.6 us
    unnamed x13, local copies, waits for them, and re-layouts  24 us
  transfers between devices with their start and end apart: 2, of which 1 were waited for; matrix products, arithmetic and copies ran while one was open for 11% of the time, Pallas kernels for 0%

profile of v1, /device:TPU:0, one launch (start us, length us, event | category | flops | bytes accessed | tf_op | source)
XLA Modules:
  0.0 672.9 jit_solution(4162792593633012166)
XLA Ops:
  0.6 0.0 copy-start
  0.6 4.6 slice_bitcast_fusion.3
  5.2 4.8 pad_maximum_fusion
  10.0 6.0 all-to-all-start.1
  16.0 23.8 %copy.17 = f32[4,128,10240]{1,0,2:T(4,128)} copy(f32[4,128,10240]{2,1,0:T(8,128)} %param.6) | data formatting | bytes 41943040 | tf_op args[0]
  39.8 0.0 copy-start.4
  39.8 0.0 copy-start.2
  39.8 0.0 copy-start.3
  39.8 92.4 %all-to-all-done.1 = bf16[4,4,128,2560]{3,2,1,0:T(8,128)(2,1)} async-done(((bf16[4,4,128,2560]{3,2,1,0:T(8,128)(2,1)}), bf16[4,4,128,2560]{3,2,1,0:T(8,128)(2,1)}, u32[]{:S(2)}, u32[]{:S(2)}) %all-to-all-start.1) | async-done | bytes 10485792 | tf_op jit(solution)/shard_map/all_to_all | solution.py:67
  132.2 7.7 %all-to-all-start = ((f32[4,128,10240]{1,0,2:T(4,128)}), f32[4,128,10240]{1,0,2:T(4,128)}, u32[]{:S(2)}, u32[]{:S(2)}) async-start(f32[4,128,10240]{1,0,2:T(4,128)} %copy.17), calls=%async_computation | async-start | bytes 41943040 | tf_op jit(solution)/shard_map/all_to_all | solution.py:65
  140.0 0.0 copy-done.4
  140.0 261.9 %all_gather.12 = f32[4,4096]{1,0:T(4,128)S(1)} all-gather(f32[4,128]{1,0:T(4,128)S(1)} %copy-done.4), channel_id=1, replica_groups=mesh['row'=8,'col'=4] {'row','col'}, dimensions={1}, use_global_device_ids=true | all-gather | bytes 67584 | tf_op jit(solution)/shard_map/all_gather | solution.py:59
  401.8 0.0 copy-done.2
  401.8 0.3 fusion.18
  402.2 0.0 copy-done.3
  402.2 37.2 %all-gather = f32[32,320,4]{1,2,0:T(4,128)S(1)} all-gather(f32[1,320,4]{1,2,0:T(4,128)S(1)} %bitcast.66), channel_id=1, replica_groups=mesh['row'=8,'col'=4] {'row','col'}, dimensions={0}, use_global_device_ids=true | all-gather | bytes 168960 | tf_op jit(solution)/shard_map/all_gather | solution.py:60
  439.4 0.1 reshape.46
  439.5 0.1 reshape.40
  439.6 0.2 fusion.10
  439.9 0.1 reshape.41
  440.0 0.0 copy-done
  440.0 0.2 dynamic-slice_reduce_fusion
  440.2 0.1 fusion.16
  440.3 9.4 %fusion.2 = (f32[4,2560]{1,0:T(4,128)S(1)}, f32[4,4,128]{2,0,1:T(4,128)S(1)}) fusion(bf16[4,4,128,2560]{3,2,1,0:T(8,128)(2,1)} %all-to-all-done.1), kind=kLoop, calls=%fused_computation.8 | loop fusion | flops 26202112 | bytes 10534912 | tf_op jit(solution)/shard_map/reduce_sum | solution.py:75
  449.7 7.4 %psum.36 = f32[4,512]{1,0:T(4,128)S(1)} all-reduce(f32[4,512]{1,0:T(4,128)S(1)} %bitcast.65), channel_id=1, replica_groups=mesh['row'=8,'col'=4] {'col'}, use_global_device_ids=true, to_apply=%region_3.0 | all-reduce | flops 2048 | bytes 16384 | tf_op jit(solution)/shard_map/psum | solution.py:74
  457.1 0.1 multiply_add_fusion.2
  457.3 33.8 %all-reduce.1 = (f32[4]{0:T(128)S(1)}, f32[4,2560]{1,0:T(4,128)S(1)}) all-reduce(f32[4]{0:T(128)S(1)} %get-tuple-element.17, f32[4,2560]{1,0:T(4,128)S(1)} %get-tuple-element.4), channel_id=1, replica_groups=mesh['row'=8,'col'=4] {'row'}, use_global_device_ids=true, to_apply=%region_8.0 | all-reduce | flops 10244 | bytes 81952 | tf_op jit(solution)/shard_map/psum | solution.py:75
  491.1 14.5 %convert_bitcast_fusion = f32[4,4,128,2560]{3,2,0,1:T(8,128)} fusion(bf16[4,4,128,2560]{3,2,1,0:T(8,128)(2,1)} %all-to-all-done.1), kind=kLoop, calls=%fused_computation.4 | loop fusion | flops 5242880 | bytes 31457280 | tf_op jit(solution)/shard_map/convert_element_type | solution.py:70
  505.6 16.5 %copy.19 = f32[4,4,128,2560]{3,2,1,0:T(8,128)} copy(f32[4,4,128,2560]{3,2,0,1:T(8,128)} %convert_bitcast_fusion) | data formatting | bytes 41943040 | tf_op jit(solution)/shard_map/convert_element_type | solution.py:70
  522.1 5.5 all_gather.15
  527.6 0.1 reshape.43
  527.7 0.2 fusion.13
  527.9 0.6 copy.45
  528.5 30.7 %all_gather.14 = f32[4,4096]{1,0:T(4,128)S(1)} all-gather(f32[4,512]{1,0:T(4,128)S(1)} %get-tuple-element.16), channel_id=1, replica_groups=mesh['row'=8,'col'=4] {'row'}, dimensions={1}, use_global_device_ids=true | all-gather | bytes 73728 | tf_op jit(solution)/shard_map/all_gather | solution.py:82
  559.2 0.7 fusion.4
  560.0 8.7 %multiply_reduce_fusion = f32[4]{0:T(128)S(1)} fusion(bf16[4,4,128,2560]{3,2,1,0:T(8,128)(2,1)} %all-to-all-done.1, f32[4]{0:T(128)S(1)} %multiply_add_fusion.3, f32[4,2560]{1,0:T(4,128)S(1)} %multiply_add_fusion.1, f32[4,4,128]{2,0,1:T(4,128)S(1)} %bitcast.63), kind=kLoop, calls=%fused_computation.5 | loop fusion | flops 31457276 | bytes 10534944 | tf_op jit(solution)/shard_map/reduce_sum | solution.py:42
  568.6 0.0 all-to-all-done
  568.6 12.6 %multiply_reduce_fusion.1 = f32[4]{0:T(128)S(1)} fusion(f32[4,4,128,2560]{2,0,3,1:T(4,128)} %bitcast.1), kind=kLoop, calls=%fused_computation.7 | loop fusion | flops 10485756 | bytes 20971536 | tf_op jit(solution)/shard_map/reduce_sum | solution.py:41
  581.3 23.9 %copy.18 = f32[4,4,128,2560]{3,2,1,0:T(8,128)} copy(f32[4,4,128,2560]{2,0,3,1:T(4,128)} %bitcast.1) | data formatting | bytes 41943040 | tf_op jit(solution)/shard_map/all_to_all | solution.py:65
  605.2 36.8 %all-reduce = (f32[4]{0:T(128)S(1)}, f32[4]{0:T(128)S(1)}) all-reduce(f32[4]{0:T(128)S(1)} %multiply_reduce_fusion, f32[4]{0:T(128)S(1)} %multiply_reduce_fusion.1), channel_id=1, replica_groups=mesh['row'=8,'col'=4] {'row','col'}, use_global_device_ids=true, to_apply=%region_10.0 | all-reduce | flops 8 | bytes 64 | tf_op jit(solution)/shard_map/psum | solution.py:34
  642.0 0.6 reduce_sum.72
  643.3 0.0 copy-start.1
  643.3 29.6 %bitcast_add_fusion = (f32[4,512,2560]{2,1,0:T(8,128)}, f32[4,512,2560]{2,1,0:T(8,128)}) fusion(f32[4,4,128,2560]{3,2,1,0:T(8,128)} %copy.18, f32[]{:T(128)S(6)} %max.3, f32[4]{0:T(128)S(1)} %multiply_add_fusion.3, f32[4,2560]{1,0:T(4,128)S(1)} %multiply_add_fusion.1, f32[4,512]{1,0:T(4,128)S(1)} %get-tuple-element.16, f32[4,4,128,2560]{3,2,1,0:T(8,128)} %copy.19, ...), kind=kLoop, calls=%fused_computation.3 | loop fusion | flops 31457280 | bytes 83935264 | tf_op jit(solution)/shard_map/add | solution.py:48
  672.9 0.0 copy-done.1
  (5 shorter events, 0.1 us)
Async XLA Ops:
  0.6 439.4 %copy-start = (s32[4,32]{1,0:T(4,128)S(1)}, s32[4,32]{1,0:T(4,128)}, u32[]{:S(2)}) copy-start(s32[4,32]{1,0:T(4,128)} %param.11) | copy-start | bytes 1540
  10.0 122.2 %all-to-all-start.1 = ((bf16[4,4,128,2560]{3,2,1,0:T(8,128)(2,1)}), bf16[4,4,128,2560]{3,2,1,0:T(8,128)(2,1)}, u32[]{:S(2)}, u32[]{:S(2)}) async-start(bf16[4,4,128,2560]{3,2,1,0:T(8,128)(2,1)} %pad_maximum_fusion), calls=%async_computation.1 | async-start | bytes 20971520 | tf_op jit(solution)/shard_map/all_to_all | solution.py:67
  39.8 100.1 %copy-start.4 = (f32[4,128]{1,0:T(4,128)S(1)}, f32[4,128]{1,0:T(4,128)}, u32[]{:S(2)}) copy-start(f32[4,128]{1,0:T(4,128)} %param.8) | copy-start | bytes 6148
  39.8 362.0 %copy-start.2 = (s32[4,32]{1,0:T(4,128)S(1)}, s32[4,32]{1,0:T(4,128)}, u32[]{:S(2)}) copy-start(s32[4,32]{1,0:T(4,128)} %param.10) | copy-start | bytes 1540
  39.8 362.3 %copy-start.3 = (f32[4,320]{1,0:T(4,128)S(1)}, f32[4,320]{1,0:T(4,128)}, u32[]{:S(2)}) copy-start(f32[4,320]{1,0:T(4,128)} %param.9) | copy-start | bytes 15364
  132.2 436.4 %all-to-all-start = ((f32[4,128,10240]{1,0,2:T(4,128)}), f32[4,128,10240]{1,0,2:T(4,128)}, u32[]{:S(2)}, u32[]{:S(2)}) async-start(f32[4,128,10240]{1,0,2:T(4,128)} %copy.17), calls=%async_computation | async-start | bytes 41943040 | tf_op jit(solution)/shard_map/all_to_all | solution.py:65
  643.3 29.6 %copy-start.1 = (s32[4,32]{1,0:T(4,128)S(1)}, s32[4,32]{1,0:T(4,128)}, u32[]{:S(2)}) copy-start(s32[4,32]{1,0:T(4,128)} %param.11) | copy-start | bytes 1540
